TPU v7x, 64 devices: a 2x2x8 block of a 4x4x8 slice. The times are simulated.
64 devices in a mesh: dp: 4 (over x, y), fsdp: 16 (over z, core).
Axes of the slice: x: 2, y: 2, z: 8, core: 2. Of those that a mesh axis runs over, the one named last changes fastest.
The devices are a block of a 4x4x8 slice.
Arguments:
- images: bfloat16 [192, 256, 1536], P(('dp', 'fsdp')), parts along dimension 0
- ln1_scale: bfloat16 [2, 1536], P(None, 'fsdp')
- ln1_bias: bfloat16 [2, 1536], P(None, 'fsdp')
- w_qkv: bfloat16 [2, 1536, 3, 16, 96], P(None, 'fsdp')
- b_qkv: bfloat16 [2, 4608], P(None, 'fsdp')
- w_out: bfloat16 [2, 1536, 1536], P(None, 'fsdp')
- b_out: bfloat16 [2, 1536], P(None, 'fsdp')
- ln2_scale: bfloat16 [2, 1536], P(None, 'fsdp')
- ln2_bias: bfloat16 [2, 1536], P(None, 'fsdp')
- w_up: bfloat16 [2, 1536, 6144], P(None, 'fsdp')
- b_up: bfloat16 [2, 6144], P(None, 'fsdp')
- w_down: bfloat16 [2, 6144, 1536], P(None, 'fsdp')
- b_down: bfloat16 [2, 1536], P(None, 'fsdp')
Outputs:
- output: bfloat16 [192, 256, 1536], P(('dp', 'fsdp')), parts along dimension 0
There are 4 independent parts. A program takes and returns all parts, laid end to end along the dimension named above; an argument that names none is the same for every part.
All inputs are finite; a program needn't handle non-finite values.
Results may differ from a plain program's by a relative error of at most 0.010846.
Values are sent between devices in bfloat16 or wider.
A program may use at most 768 MiB of HBM per device.

v0:
```python
import jax
import jax.numpy as jnp
from jax import lax
from jax.sharding import PartitionSpec as P

LN_EPS = 1e-6
WEIGHT_NAMES = ('ln1_scale', 'ln1_bias', 'w_qkv', 'b_qkv', 'w_out', 'b_out', 'ln2_scale', 'ln2_bias', 'w_up', 'b_up', 'w_down', 'b_down')


def layer_norm(values, ln_scale, ln_shift):
    centered = values.astype(jnp.float32)
    centered = centered - jnp.mean(centered, axis=-1, keepdims=True)
    variance = jnp.mean(jnp.square(centered), axis=-1, keepdims=True)
    normed = centered * lax.rsqrt(variance + LN_EPS)
    return (normed * ln_scale.astype(jnp.float32) + ln_shift.astype(jnp.float32)).astype(jnp.bfloat16)


def attention_heads(queries, key_heads, values):
    score_scale = queries.shape[-1] ** -0.5

    def one_head(operands):
        q_head, k_head, v_head = operands
        scores = jnp.einsum('crf,clf->crl', q_head, k_head, preferred_element_type=jnp.float32) * score_scale
        attn_probs = jax.nn.softmax(scores, axis=-1).astype(jnp.bfloat16)
        return jnp.einsum('crl,clf->crf', attn_probs, v_head, preferred_element_type=jnp.float32).astype(jnp.bfloat16)

    return lax.map(one_head, (queries, key_heads, values))


def encoder_layer(tokens, fetch):
    normed = layer_norm(tokens, fetch('ln1_scale'), fetch('ln1_bias'))
    w_qkv = fetch('w_qkv')
    width, num_heads, head_dim = w_qkv.shape[0], w_qkv.shape[2], w_qkv.shape[3]
    qkv_heads = jnp.einsum('btd,dche->chbte', normed, w_qkv, preferred_element_type=jnp.float32)
    qkv_bias = fetch('b_qkv').astype(jnp.float32).reshape(3, num_heads, 1, 1, head_dim)
    qkv_heads = (qkv_heads + qkv_bias).astype(jnp.bfloat16)
    attended = attention_heads(qkv_heads[0], qkv_heads[1], qkv_heads[2])
    w_out = fetch('w_out').reshape(num_heads, head_dim, width)
    projected = jnp.einsum('hbte,hed->btd', attended, w_out, preferred_element_type=jnp.float32)
    after_attn = (tokens.astype(jnp.float32) + projected + fetch('b_out').astype(jnp.float32)).astype(jnp.bfloat16)
    normed_mlp = layer_norm(after_attn, fetch('ln2_scale'), fetch('ln2_bias'))
    hidden = jnp.einsum('btd,df->btf', normed_mlp, fetch('w_up'), preferred_element_type=jnp.float32) + fetch('b_up').astype(jnp.float32)
    gelu_out = jax.nn.gelu(hidden, approximate=True).astype(jnp.bfloat16)
    down_proj = jnp.einsum('btf,fd->btd', gelu_out, fetch('w_down'), preferred_element_type=jnp.float32)
    return (after_attn.astype(jnp.float32) + down_proj + fetch('b_down').astype(jnp.float32)).astype(jnp.bfloat16)


def solution(mesh):
    batch_spec = P(('dp', 'fsdp'), None, None)
    vector_spec = P(None, 'fsdp')
    matrix_spec = P(None, 'fsdp', None)
    weight_specs = (vector_spec, vector_spec, P(None, 'fsdp', None, None, None), vector_spec, matrix_spec, vector_spec,
                    vector_spec, vector_spec, matrix_spec, vector_spec, matrix_spec, vector_spec)

    def local_forward(tokens, *shards):
        stored = dict(zip(WEIGHT_NAMES, shards))
        for layer in range(shards[0].shape[0]):
            def fetch(name, layer=layer):
                return lax.all_gather(stored[name][layer], 'fsdp', axis=0, tiled=True)
            tokens = encoder_layer(tokens, fetch)
        return tokens

    return jax.shard_map(local_forward, mesh=mesh, in_specs=(batch_spec,) + weight_specs, out_specs=batch_spec, check_vma=False)
```

profile of v0, /device:TPU:21, one launch (start us, length us, event | category | flops | bytes accessed | tf_op | source)
XLA Modules:
  0.0 737.0 jit_solution(14916664501808042350)
XLA Ops:
  6.6 3.6 slice_bitcast_fusion.6
  13.9 3.4 fusion.225
  24.9 56.3 %all-reduce.14 = (bf16[4608]{0:T(1024)(128)(2,1)S(1)}, bf16[4608]{0:T(1024)(128)(2,1)S(1)}, bf16[1536]{0:T(1024)(128)(2,1)S(1)}, bf16[1536]{0:T(1024)(128)(2,1)S...) all-reduce(bf16[4608]{0:T(1024)(128)(2,1)S(1)} %dynamic-update-slic, ...), channel_id=5, replica_groups=mesh['dp'=4,'fsdp'=16] {'fsdp'}, use_global_device_ids=true, to_apply=%add.2 | all-reduce | flops 27648 | bytes 110592
  81.4 18.5 %all-gather.9 = bf16[1,6144]{1,0:T(2,128)(2,1)S(1)} all-gather(bf16[1,384]{1,0:T(2,128)(2,1)S(1)} %get-tuple-element.132), channel_id=11, replica_groups=mesh['dp'=4,'fsdp'=16] {'fsdp'}, dimensions={1}, use_global_device_ids=true | all-gather | bytes 13056 | tf_op jit(solution)/shard_map/all_gather | solution.py:59
  101.9 16.7 %all-gather.21 = bf16[1,6144]{1,0:T(2,128)(2,1)S(1)} all-gather(bf16[1,384]{1,0:T(2,128)(2,1)S(1)} %get-tuple-element.131), channel_id=23, replica_groups=mesh['dp'=4,'fsdp'=16] {'fsdp'}, dimensions={1}, use_global_device_ids=true | all-gather | bytes 13056 | tf_op jit(solution)/shard_map/all_gather | solution.py:59
  121.0 23.2 %copy.29 = bf16[1,1536,3,16,96]{1,4,3,2,0:T(8,128)(2,1)} copy(bf16[1,1536,3,16,96]{4,3,2,0,1:T(8,128)(2,1)} %all-gather.33.cloned.1.call-done) | data formatting | bytes 28311552 | tf_op jit(solution)/shard_map/all_gather | solution.py:59
  144.3 76.7 %all-gather.41.cloned.1.call-done = bf16[1,1536,3,16,96]{4,3,2,0,1:T(8,128)(2,1)} async-done(((bf16[1,96,3,16,96]{4,3,2,0,1:T(8,128)(2,1)}), bf16[1,1536,3,16,96]{4,3,2,0,1:T(8,128)(2,1)}) %all-gather.41.cloned.1.call-update) | async-done | bytes 14155792 | tf_op jit(solution)/shard_map/all_gather | solution.py:59
  221.0 23.2 %copy.35 = bf16[1,1536,3,16,96]{1,4,3,2,0:T(8,128)(2,1)} copy(bf16[1,1536,3,16,96]{4,3,2,0,1:T(8,128)(2,1)} %all-gather.41.cloned.1.call-done) | data formatting | bytes 28311552 | tf_op jit(solution)/shard_map/all_gather | solution.py:59
  244.2 15.0 %fusion.160 = bf16[3,16,3,256,96]{3,4,1,0,2:T(8,128)(2,1)S(1)} fusion(f32[3,16,96]{2,1,0:T(8,128)S(1)} %reshape.78, bf16[1,1536,3,16,96]{1,4,3,2,0:T(8,128)(2,1)} %copy.29, bf16[3,256,1536]{2,1,0:T(8,128)(2,1)S(1)} %copy-done, f32[1536]{0:T(1024)S(1)} %convert_element_type.161, f32[1536]{0:T(1024)S(1)} %convert_element_type.160, ...), kind=kOutput, calls=%fused_computation.130 | convolution fusion | flops 10885791744 | bytes 23629824 | tf_op jit(solution)/shard_map/btd,dche->chbte/dot_general | solution.py:34
  259.2 3.0 slice_bitcast_fusion.3
  263.9 60.2 %while.20 = (s32[]{:T(128)}, bf16[16,3,256,96]{2,3,1,0:T(8,128)(2,1)}, bf16[16,3,256,96]{2,3,0,1:T(8,128)(2,1)}, bf16[16,3,256,96]{2,3,0,1:T(8,128)(2,1)}, bf16[16,3,256,96]{2,3,0,1:T(8,128)(2,1)}, /*index=5*/s32[]{:T(128)}) while((s32[]{:T(128)}, bf16[16,3,256,96]{2,3,1,0:T(8,128)(2,1)}, bf16[16,3,256,96]{2,3,0,1:T(8,128)(2,1)}, ...), condition=%wide.region_5.6_spmd, body=%wide.region_2.5_spmd.sunk | while | flops 114697472 | bytes 894021 | solution.py:27
  265.3 2.3 fusion.271
  269.1 2.3 fusion.271
  272.8 2.3 fusion.271
  276.6 2.3 fusion.271
  280.3 2.3 fusion.271
  284.1 2.3 fusion.271
  287.8 2.3 fusion.271
  291.6 2.3 fusion.271
  295.3 2.3 fusion.271
  299.1 2.3 fusion.271
  302.8 2.3 fusion.271
  306.6 2.3 fusion.271
  310.3 2.3 fusion.271
  314.1 2.3 fusion.271
  317.8 2.3 fusion.271
  321.6 2.3 fusion.271
  324.1 7.3 convert_reduce_fusion.2
  333.6 28.8 %all-gather.37.cloned.1.call-done = bf16[1,1536,6144]{2,1,0:T(8,128)(2,1)} async-done(((bf16[1,96,6144]{2,1,0:T(8,128)(2,1)}), bf16[1,1536,6144]{2,1,0:T(8,128)(2,1)}) %all-gather.37.cloned.1.call-update) | async-done | bytes 18874384 | tf_op jit(solution)/shard_map/all_gather | solution.py:59
  362.4 26.0 %fusion.85.clone.3.clone.4 = bf16[3,256,6144]{2,1,0:T(8,128)(2,1)} fusion(bf16[1,1536,6144]{2,1,0:T(8,128)(2,1)} %all-gather.37.cloned.1.call-done, f32[6144]{0:T(1024)S(1)} %bitcast.241, bf16[3,256,1536]{2,1,0:T(8,128)(2,1)} %copy-done.3, f32[1536]{0:T(1024)S(1)} %convert_element_type.164, ...), kind=kOutput, calls=%fused_computation.53.clone.clone.clone.clone.clone.clone.clone.1 | convolution fusion | flops 14549778432 | bytes 30713856 | tf_op jit(solution)/shard_map/btd,df->btf/dot_general | solution.py:42
  388.4 76.1 %all-gather.39.cloned.1.call-done = bf16[1,6144,1536]{2,1,0:T(8,128)(2,1)} async-done(((bf16[1,384,1536]{2,1,0:T(8,128)(2,1)}), bf16[1,6144,1536]{2,1,0:T(8,128)(2,1)}) %all-gather.39.cloned.1.call-update) | async-done | bytes 18874384 | tf_op jit(solution)/shard_map/all_gather | solution.py:59
  464.4 21.2 %convert_reduce_fusion.1 = (f32[3,256]{1,0:T(4,128)S(1)}, bf16[3,256,1536]{2,1,0:T(8,128)(2,1)S(1)}) fusion(f32[1536]{0:T(1024)S(1)} %convert_element_type.165, bf16[1,6144,1536]{2,1,0:T(8,128)(2,1)} %all-gather.39.cloned.1.call-done, bf16[3,256,1536]{2,1,0:T(8,128)(2,1)S(1)} %copy-done.4, bf16[3,256,6144]{2,1,0:T(8,128)(2,1)} %fusion.85.clone.3.clone.4), kind=kOutput, calls=%fused_computation.91 | convolution fusion | flops 14502591488 | bytes 33039360 | tf_op jit(solution)/shard_map/btf,fd->btd/dot_general | solution.py:44
  486.4 15.2 %fusion.163 = bf16[3,16,3,256,96]{3,4,1,0,2:T(8,128)(2,1)S(1)} fusion(f32[3,16,96]{2,1,0:T(8,128)S(1)} %reshape.79, bf16[1,1536,3,16,96]{1,4,3,2,0:T(8,128)(2,1)} %copy.35, bf16[3,256,1536]{2,1,0:T(8,128)(2,1)S(1)} %get-tuple-element.148, f32[1536]{0:T(1024)S(1)} %convert_element_type.167, f32[1536]{0:T(1024)S(1)} %convert_element_type.166, ...), kind=kOutput, calls=%fused_computation.131 | convolution fusion | flops 10885791744 | bytes 23629824 | tf_op jit(solution)/shard_map/btd,dche->chbte/dot_general | solution.py:34
  501.6 2.9 slice_bitcast_fusion
  506.2 59.1 %while.21 = (s32[]{:T(128)}, bf16[16,3,256,96]{2,3,1,0:T(8,128)(2,1)}, bf16[16,3,256,96]{2,3,0,1:T(8,128)(2,1)}, bf16[16,3,256,96]{2,3,0,1:T(8,128)(2,1)}, bf16[16,3,256,96]{2,3,0,1:T(8,128)(2,1)S(1)}, /*index=5*/s32[]{:T(128)}) while((s32[]{:T(128)}, bf16[16,3,256,96]{2,3,1,0:T(8,128)(2,1)}, bf16[16,3,256,96]{2,3,0,1:T(8,128)(2,1)}, ...), condition=%wide.region_13.14_spmd, body=%wide.region_10.13_spmd.sunk | while | flops 114697472 | bytes 895045 | solution.py:27
  507.6 2.3 fusion.278
  515.0 2.3 fusion.278
  522.4 2.3 fusion.278
  529.7 2.3 fusion.278
  537.1 2.3 fusion.278
  544.4 2.3 fusion.278
  551.8 2.3 fusion.278
  559.2 2.3 fusion.278
  565.4 8.1 %convert_reduce_fusion = (f32[3,256]{1,0:T(4,128)S(1)}, bf16[3,256,1536]{2,1,0:T(8,128)(2,1)S(1)}) fusion(f32[1536]{0:T(1024)S(1)} %copy-done.10, bf16[16,3,256,96]{2,3,1,0:T(8,128)(2,1)} %get-tuple-element.60, bf16[16,96,1536,1]{2,1,3,0:T(8,128)(2,1)} %bitcast.242, bf16[3,256,1536]{2,1,0:T(8,128)(2,1)} %copy-done.2), kind=kOutput, calls=%fused_computation.88 | convolution fusion | flops 3630955776 | bytes 11805696 | tf_op jit(solution)/shard_map/hbte,hed->btd/dot_general | solution.py:39
  574.2 31.6 %all-gather.45.cloned.1.call-done = bf16[1,1536,6144]{2,1,0:T(8,128)(2,1)} async-done(((bf16[1,96,6144]{2,1,0:T(8,128)(2,1)}), bf16[1,1536,6144]{2,1,0:T(8,128)(2,1)}) %all-gather.45.cloned.1.call-update) | async-done | bytes 18874384 | tf_op jit(solution)/shard_map/all_gather | solution.py:59
  605.8 23.7 %fusion.93.clone.6 = bf16[3,256,6144]{2,1,0:T(8,128)(2,1)} fusion(bf16[1,1536,6144]{2,1,0:T(8,128)(2,1)} %all-gather.45.cloned.1.call-done, f32[6144]{0:T(1024)S(1)} %bitcast.240, bf16[3,256,1536]{2,1,0:T(8,128)(2,1)S(1)} %get-tuple-element.150, f32[1536]{0:T(1024)S(1)} %copy-done.9, f32[1536]{0:T(1024)S(1)} %copy-done.8, ...), kind=kOutput, calls=%fused_computation.61.clone.clone.clone.clone.clone.1 | convolution fusion | flops 14549778432 | bytes 30713856 | tf_op jit(solution)/shard_map/btd,df->btf/dot_general | solution.py:42
  629.5 78.4 %all-gather.47.cloned.1.call-done = bf16[1,6144,1536]{2,1,0:T(8,128)(2,1)} async-done(((bf16[1,384,1536]{2,1,0:T(8,128)(2,1)}), bf16[1,6144,1536]{2,1,0:T(8,128)(2,1)}) %all-gather.47.cloned.1.call-update) | async-done | bytes 18874384 | tf_op jit(solution)/shard_map/all_gather | solution.py:59
  707.9 21.8 %fusion.159 = bf16[3,256,1536]{2,1,0:T(8,128)(2,1)} fusion(bf16[3,256,1536]{2,1,0:T(8,128)(2,1)S(1)} %get-tuple-element.150, bf16[1,6144,1536]{2,1,0:T(8,128)(2,1)} %all-gather.47.cloned.1.call-done, f32[1536]{0:T(1024)S(1)} %copy-done.7, bf16[3,256,6144]{2,1,0:T(8,128)(2,1)} %fusion.93.clone.6), kind=kOutput, calls=%fused_computation.129 | convolution fusion | flops 14500233216 | bytes 33036288 | tf_op jit(solution)/shard_map/btf,fd->btd/dot_general | solution.py:44
  (169 shorter events, 85.1 us)
Async XLA Ops:
  6.5 4.5 copy-start.5
  6.5 5.5 copy-start.1
  6.6 114.5 %all-gather.33.cloned.1.call-start = ((), (), s32[]{:S(2)}) async-start(), calls=%async_computation | async-start | bytes 20054016 | tf_op jit(solution)/shard_map/all_gather | solution.py:59
  10.2 210.8 %all-gather.41.cloned.1.call-start = ((), (), s32[]{:S(2)}) async-start(), calls=%async_computation.4 | async-start | bytes 20054016 | tf_op jit(solution)/shard_map/all_gather | solution.py:59
  11.0 313.1 %all-gather.35.cloned.1.call-start = ((), (), s32[]{:S(2)}) async-start(), calls=%async_computation.1 | async-start | bytes 5013504 | tf_op jit(solution)/shard_map/all_gather | solution.py:59
  12.0 350.4 %all-gather.37.cloned.1.call-start = ((), (), s32[]{:S(2)}) async-start(), calls=%async_computation.2 | async-start | bytes 20054016 | tf_op jit(solution)/shard_map/all_gather | solution.py:59
  13.7 5.9 copy-start.19
  13.7 7.8 %copy-start.13 = (bf16[2,96]{1,0:T(2,128)(2,1)S(1)}, bf16[2,96]{1,0:T(2,128)(2,1)}, u32[]{:S(2)}) copy-start(bf16[2,96]{1,0:T(2,128)(2,1)} %param.18) | copy-start | bytes 1156
  13.7 8.1 %copy-start.14 = (bf16[2,96]{1,0:T(2,128)(2,1)S(1)}, bf16[2,96]{1,0:T(2,128)(2,1)}, u32[]{:S(2)}) copy-start(bf16[2,96]{1,0:T(2,128)(2,1)} %param.19) | copy-start | bytes 1156
  13.7 8.3 %copy-start.15 = (bf16[2,96]{1,0:T(2,128)(2,1)S(1)}, bf16[2,96]{1,0:T(2,128)(2,1)}, u32[]{:S(2)}) copy-start(bf16[2,96]{1,0:T(2,128)(2,1)} %param.23) | copy-start | bytes 1156
  13.7 8.6 %copy-start.16 = (bf16[2,96]{1,0:T(2,128)(2,1)S(1)}, bf16[2,96]{1,0:T(2,128)(2,1)}, u32[]{:S(2)}) copy-start(bf16[2,96]{1,0:T(2,128)(2,1)} %param.24) | copy-start | bytes 1156
  13.7 8.9 %copy-start.17 = (bf16[2,96]{1,0:T(2,128)(2,1)S(1)}, bf16[2,96]{1,0:T(2,128)(2,1)}, u32[]{:S(2)}) copy-start(bf16[2,96]{1,0:T(2,128)(2,1)} %param.25) | copy-start | bytes 1156
  13.7 9.1 %copy-start.18 = (bf16[2,96]{1,0:T(2,128)(2,1)S(1)}, bf16[2,96]{1,0:T(2,128)(2,1)}, u32[]{:S(2)}) copy-start(bf16[2,96]{1,0:T(2,128)(2,1)} %param.29) | copy-start | bytes 1156
  13.7 10.7 %copy-start.11 = (bf16[2,288]{1,0:T(2,128)(2,1)S(1)}, bf16[2,288]{1,0:T(2,128)(2,1)}, u32[]{:S(2)}) copy-start(bf16[2,288]{1,0:T(2,128)(2,1)} %param.21) | copy-start | bytes 3460
  13.8 67.6 %copy-start.12 = (bf16[2,384]{1,0:T(2,128)(2,1)S(1)}, bf16[2,384]{1,0:T(2,128)(2,1)}, u32[]{:S(2)}) copy-start(bf16[2,384]{1,0:T(2,128)(2,1)} %param.27) | copy-start | bytes 4612
  13.8 106.0 %copy-start = (bf16[3,256,1536]{2,1,0:T(8,128)(2,1)S(1)}, bf16[3,256,1536]{2,1,0:T(8,128)(2,1)}, u32[]{:S(2)}) copy-start(bf16[3,256,1536]{2,1,0:T(8,128)(2,1)} %param.17) | copy-start | bytes 7077892
  13.8 450.6 %all-gather.39.cloned.1.call-start = ((), (), s32[]{:S(2)}) async-start(), calls=%async_computation.3 | async-start | bytes 20054016 | tf_op jit(solution)/shard_map/all_gather | solution.py:59
  17.3 548.0 %all-gather.43.cloned.1.call-start = ((), (), s32[]{:S(2)}) async-start(), calls=%async_computation.5 | async-start | bytes 5013504 | tf_op jit(solution)/shard_map/all_gather | solution.py:59
  18.0 587.9 %all-gather.45.cloned.1.call-start = ((), (), s32[]{:S(2)}) async-start(), calls=%async_computation.6 | async-start | bytes 20054016 | tf_op jit(solution)/shard_map/all_gather | solution.py:59
  18.8 689.1 %all-gather.47.cloned.1.call-start = ((), (), s32[]{:S(2)}) async-start(), calls=%async_computation.7 | async-start | bytes 20054016 | tf_op jit(solution)/shard_map/all_gather | solution.py:59
  331.4 1.4 copy-start.3
  362.4 102.0 %copy-start.4 = (bf16[3,256,1536]{2,1,0:T(8,128)(2,1)S(1)}, bf16[3,256,1536]{2,1,0:T(8,128)(2,1)}, u32[]{:S(2)}) copy-start(bf16[3,256,1536]{2,1,0:T(8,128)(2,1)} %copy-done.3) | copy-start | bytes 7077892
  485.6 16.0 %copy-start.2 = (bf16[3,256,1536]{2,1,0:T(8,128)(2,1)}, bf16[3,256,1536]{2,1,0:T(8,128)(2,1)S(1)}, u32[]{:S(2)}) copy-start(bf16[3,256,1536]{2,1,0:T(8,128)(2,1)S(1)} %get-tuple-element.148) | copy-start | bytes 7077892
  506.2 59.2 %copy-start.10 = (f32[1536]{0:T(1024)S(1)}, f32[1536]{0:T(1024)}, u32[]{:S(2)}) copy-start(f32[1536]{0:T(1024)} %convert_element_type.168) | copy-start | bytes 18436
  565.4 40.4 %copy-start.6 = (f32[1,6144]{1,0:T(1,128)S(1)}, f32[1,6144]{1,0:T(1,128)}, u32[]{:S(2)}) copy-start(f32[1,6144]{1,0:T(1,128)} %convert_element_type.158) | copy-start | bytes 73732
  565.4 40.4 %copy-start.8 = (f32[1536]{0:T(1024)S(1)}, f32[1536]{0:T(1024)}, u32[]{:S(2)}) copy-start(f32[1536]{0:T(1024)} %convert_element_type.169) | copy-start | bytes 18436
  565.4 40.4 %copy-start.9 = (f32[1536]{0:T(1024)S(1)}, f32[1536]{0:T(1024)}, u32[]{:S(2)}) copy-start(f32[1536]{0:T(1024)} %convert_element_type.170) | copy-start | bytes 18436
  605.8 102.1 %copy-start.7 = (f32[1536]{0:T(1024)S(1)}, f32[1536]{0:T(1024)}, u32[]{:S(2)}) copy-start(f32[1536]{0:T(1024)} %convert_element_type.171) | copy-start | bytes 18436
Sparse Core Ops, SparseCore 0:
  10.3 108.4 all-gather.32
  120.5 100.4 all-gather.40
  222.6 37.5 all-gather.34
  261.7 100.6 all-gather.36
  363.9 100.5 all-gather.38
  465.9 37.5 all-gather.42
  505.1 100.6 all-gather.44
  607.4 100.4 all-gather.46
where the time goes:
time: 745 us; the launch traced here: 737 us
  waiting for transfers between devices  295 us (40%)
  matrix products  257 us (34%)
  blocking collectives  91.6 us (12%)
  local copies, waits for them, and re-layouts  70.7 us (9%)
  between operations  15.7 us (2%)
    all_gather x8, waiting for transfers between devices, fetch(): return lax.all_gather(stored[name][layer], 'fsdp', axis=0, tiled=True)  292 us
    dot_general x32, matrix products, one_head(): jnp.einsum('crl,clf->crf', attn_probs, v_head, preferred_element_type=jnp...  73.3 us
    unnamed x1, blocking collectives  56.3 us
    dot_general x2, matrix products, encoder_layer(): jnp.einsum('btd,df->btf', normed_mlp, fetch('w_up'), preferred_element_ty...  49.7 us
    all_gather x2, local copies, waits for them, and re-layouts, fetch(): return lax.all_gather(stored[name][layer], 'fsdp', axis=0, tiled=True)  46.4 us
    sub x32, matrix products, one_head(): attn_probs = jax.nn.softmax(scores, axis=-1).astype(jnp.bfloat16)  45.5 us
    dot_general x2, matrix products, encoder_layer(): jnp.einsum('btf,fd->btd', gelu_out, fetch('w_down'), preferred_element_ty...  43 us
    all_gather x2, blocking collectives, fetch(): return lax.all_gather(stored[name][layer], 'fsdp', axis=0, tiled=True)  35.3 us
  transfers between devices with their start and end apart: 8, of which 5 were waited for; matrix products, arithmetic and copies ran while one was open for 42% of the time, Pallas kernels for 0%

commit v1 on v0

v1 whole, which is shorter than its diff:
```python
import functools
import math

import jax
import jax.numpy as jnp
from jax import lax
from jax.experimental import pallas as pl
from jax.experimental.pallas import tpu as pltpu
from jax.sharding import PartitionSpec as P

LN_EPS = 1e-6
MESH = pl.DeviceIdType.MESH
CORES = 2
SUB = 3
COMPUTE = True

LN1_S, LN1_B, B_QKV, B_OUT, LN2_S, LN2_B, B_UP, B_DOWN = range(8)
QKV, OUT, UP, DOWN = range(4)
GROUPS = (((0, QKV),), ((0, OUT), (0, UP)), ((0, DOWN),), ((1, QKV), (1, OUT)), ((1, UP),), ((1, DOWN),))
F32 = jnp.float32
BF16 = jnp.bfloat16


def _kernel(dims, x_in, vec_in, *refs):
    ny, nz, heads, hd = dims
    win, refs = refs[:4], refs[4:]
    out_ref, refs = refs[0], refs[1:]
    gath, refs = refs[:4], refs[4:]
    x, h, qkv, g, acc, wt = refs[:6]
    bounce, refs = refs[6:10], refs[10:]
    vecg, vrow = refs[:2]
    (rec_a, rec_b, rec_x, rec_y, rec_d, rec_l, snd_a, snd_b, snd_x, snd_y, snd_d, snd_v, vec_a, vec_b, vec_d, loc, tile_sem,
     out_sem) = refs[2:]

    rows, width = x.shape
    mblocks = 3
    mrows = rows // mblocks
    steps = nz - 1
    ticks = steps * SUB

    d = lax.axis_index('dp')
    f = lax.axis_index('fsdp')
    z, c = f // CORES, f % CORES
    up_dev = (d, ((z + 1) % nz) * CORES + c)
    dn_dev = (d, ((z + nz - 1) % nz) * CORES + c)
    sib_dev = (d, z * CORES + (CORES - 1 - c))
    x_dev = (d + ny * (1 - 2 * ((d // ny) % 2)), f)
    y_dev = (d + 1 - 2 * (d % 2), f)
    par = (d // ny + d % ny) % 2
    qa, qb = 2 * par, 2 * par + 1
    qx, qy = 2 * (1 - par), 2 * (1 - par) + 1

    barrier = pltpu.get_barrier_semaphore()
    for dev in (up_dev, dn_dev, sib_dev, x_dev, y_dev):
        pl.semaphore_signal(barrier, inc=1, device_id=dev, device_id_type=MESH)
    pl.semaphore_wait(barrier, 5)

    def remote(src, dst, ssem, rsem, dev):
        return pltpu.make_async_remote_copy(src_ref=src, dst_ref=dst, send_sem=ssem, recv_sem=rsem, device_id=dev,
                                            device_id_type=MESH)

    def wid(w):
        return w[0] * 4 + w[1]

    def shard_rows(kind):
        return win[kind].shape[1]

    def part(ref, w, origin, q, j):
        l, kind = w
        r = shard_rows(kind)
        if kind == DOWN:
            n = r // SUB
            cols = ref.shape[2] // 4
            return ref.at[l, pl.ds(pl.multiple_of(origin * r + j * n, 8), n), pl.ds(pl.multiple_of(q * cols, 128), cols)]
        n = r // (4 * SUB)
        return ref.at[l, pl.ds(pl.multiple_of(origin * r + q * (r // 4) + j * n, 8), n), :]

    def amount(w, quarters):
        l, kind = w
        r, cols = shard_rows(kind), gath[kind].shape[2]
        if kind == DOWN and quarters % 4:
            return gath[kind].at[l, pl.ds(0, quarters * r), pl.ds(0, cols // 4)]
        return gath[kind].at[l, pl.ds(0, quarters * (r // 4)), :]

    def wait_bytes(view, sem):
        pltpu.make_async_copy(view, view, sem).wait()

    def d2d_sem(w, t):
        return rec_l.at[t] if w == GROUPS[-1][-1] else rec_d.at[wid(w)]

    def own_send(grp, j):
        for w in GROUPS[grp]:
            l, kind = w
            remote(part(win[kind], w, 0, qa, j), part(gath[kind], w, f, qa, j), snd_a.at[wid(w)], rec_a.at[wid(w), 0, j], up_dev).start()
            remote(part(win[kind], w, 0, qb, j), part(gath[kind], w, f, qb, j), snd_b.at[wid(w)], rec_b.at[wid(w), 0, j], dn_dev).start()

    def own_d2d(grp):
        for w in GROUPS[grp]:
            l, kind = w
            r = shard_rows(kind)
            remote(win[kind].at[l], gath[kind].at[l, pl.ds(pl.multiple_of(f * r, 8), r), :], snd_d.at[wid(w)], d2d_sem(w, 0), sib_dev).start()

    def xy_arrive(grp, t, j):
        oa = ((z - t + nz) % nz) * CORES + c
        ob = ((z + t) % nz) * CORES + c
        for w in GROUPS[grp]:
            l, kind = w
            px, py = part(gath[kind], w, oa, qx, j), part(gath[kind], w, ob, qy, j)
            remote(px, px, snd_x.at[wid(w)], rec_x.at[wid(w), t - 1, j], x_dev).wait_recv()
            remote(px, px, snd_d.at[wid(w)], d2d_sem(w, t), sib_dev).start()
            remote(py, py, snd_y.at[wid(w)], rec_y.at[wid(w), t - 1, j], y_dev).wait_recv()
            remote(py, py, snd_d.at[wid(w)], d2d_sem(w, t), sib_dev).start()

    def tick(grp, i, early):
        t, j = i // SUB + 1, i % SUB
        oa = ((z - t + nz) % nz) * CORES + c
        ob = ((z + t) % nz) * CORES + c
        for w in GROUPS[grp]:
            l, kind = w
            for o, q, snd, rec, dev in ((oa, qa, snd_a, rec_a, up_dev), (ob, qb, snd_b, rec_b, dn_dev)):
                p = part(gath[kind], w, o, q, j)
                remote(p, p, snd.at[wid(w)], rec.at[wid(w), t - 1, j], dev).wait_recv()

                @pl.when(t < steps)
                def _():
                    remote(p, p, snd.at[wid(w)], rec.at[wid(w), t, j], dev).start()

            pa, pb = part(gath[kind], w, oa, qa, j), part(gath[kind], w, ob, qb, j)
            remote(pa, pa, snd_x.at[wid(w)], rec_x.at[wid(w), t - 1, j], x_dev).start()
            remote(pb, pb, snd_y.at[wid(w)], rec_y.at[wid(w), t - 1, j], y_dev).start()
            remote(pa, pa, snd_d.at[wid(w)], d2d_sem(w, t), sib_dev).start()
            remote(pb, pb, snd_d.at[wid(w)], d2d_sem(w, t), sib_dev).start()
        if grp + 1 < len(GROUPS):

            @pl.when(t == steps - 1)
            def _():
                own_send(grp + 1, j)

        if grp == 0:
            half = nz // 2
            va, vb = vecg.at[oa], vecg.at[ob]

            @pl.when(jnp.logical_and(j == 0, t <= half))
            def _():
                remote(va, va, snd_v.at[0], vec_a.at[t - 1], up_dev).wait_recv()

                @pl.when(t < half)
                def _():
                    remote(va, va, snd_v.at[0], vec_a.at[t], up_dev).start()

                remote(va, va, snd_v.at[2], vec_d, sib_dev).start()

            @pl.when(jnp.logical_and(j == 0, t < half))
            def _():
                remote(vb, vb, snd_v.at[1], vec_b.at[t - 1], dn_dev).wait_recv()

                @pl.when(t < half - 1)
                def _():
                    remote(vb, vb, snd_v.at[1], vec_b.at[t], dn_dev).start()

                remote(vb, vb, snd_v.at[2], vec_d, sib_dev).start()

        if not early:
            xy_arrive(grp, t - 1, j)
        elif grp > 0:
            xy_arrive(grp - 1, steps, j)

    def run(grp, lo, hi, total=0, unit=None):
        def body(i, carry):
            tick(grp, i, hi <= SUB)
            if unit is not None and COMPUTE:
                k = i - lo
                lax.fori_loop((k * total) // (hi - lo), ((k + 1) * total) // (hi - lo), lambda u, cc: (unit(u), cc)[1], 0)
            return carry

        lax.fori_loop(lo, hi, body, 0)

    def await_group(grp):
        for w in GROUPS[grp]:
            wait_bytes(amount(w, 4 * nz), rec_d.at[wid(w)])

    def vec(l, k, n, width_):
        return vrow[pl.ds(l * 8 + k, 1), pl.ds(n, width_)]

    def ln_unit(l, ks, kb):
        n = 64

        def unit(u):
            sl = pl.ds(pl.multiple_of(u * n, n), n)
            v = x[sl, :].astype(F32)
            v = v - jnp.mean(v, axis=-1, keepdims=True)
            var = jnp.mean(v * v, axis=-1, keepdims=True)
            y = v * lax.rsqrt(var + LN_EPS)
            h[sl, :] = (y * vec(l, ks, 0, width) + vec(l, kb, 0, width)).astype(BF16)

        return rows // n, unit

    kt, nt = wt.shape[1], wt.shape[2]

    def tile_copy(w, i, kparts):
        l, kind = w
        n, k = i // kparts, i % kparts
        src = gath[kind].at[l, pl.ds(pl.multiple_of(k * kt, 8), kt), pl.ds(pl.multiple_of(n * nt, 128), nt)]
        return pltpu.make_async_copy(src, wt.at[i % 2], tile_sem.at[i % 2])

    def mm_unit(w, a_ref, epilogue):
        l, kind = w
        kparts = (gath[kind].shape[1]) // kt
        ntiles = gath[kind].shape[2] // nt * kparts

        def unit(u):
            i, mb = u // mblocks, u % mblocks
            n, k = i // kparts, i % kparts

            @pl.when(mb == 0)
            def _():
                tile_copy(w, i, kparts).wait()

                @pl.when(i + 1 < ntiles)
                def _():
                    tile_copy(w, i + 1, kparts).start()

            msl = pl.ds(pl.multiple_of(mb * mrows, mrows), mrows)
            nsl = pl.ds(pl.multiple_of(n * nt, 128), nt)
            ksl = pl.ds(pl.multiple_of(k * kt, 128), kt) if kparts > 1 else slice(None)
            res = jnp.dot(a_ref[msl, ksl], wt[i % 2], preferred_element_type=F32)
            epilogue(res, msl, nsl, n * nt, k)

        return ntiles * mblocks, unit, functools.partial(lambda: tile_copy(w, 0, kparts).start())

    def lanes(n):
        return pl.multiple_of(n, 128)

    def qkv_epi(l):
        def epi(res, msl, nsl, n0, k):
            qkv[msl, nsl] = (res + vec(l, B_QKV, lanes(n0), nt)).astype(BF16)

        return epi

    def out_epi(l):
        def epi(res, msl, nsl, n0, k):
            x[msl, nsl] = (x[msl, nsl].astype(F32) + (res + vec(l, B_OUT, lanes(n0), nt))).astype(BF16)

        return epi

    def up_epi(l):
        def epi(res, msl, nsl, n0, k):
            g[msl, nsl] = jax.nn.gelu(res + vec(l, B_UP, lanes(n0), nt), approximate=True).astype(BF16)

        return epi

    def down_epi(l, kparts):
        def epi(res, msl, nsl, n0, k):
            @pl.when(k == 0)
            def _():
                acc[msl, nsl] = res

            @pl.when(jnp.logical_and(k > 0, k < kparts - 1))
            def _():
                acc[msl, nsl] += res

            @pl.when(k == kparts - 1)
            def _():
                x[msl, nsl] = (x[msl, nsl].astype(F32) + (acc[msl, nsl] + res + vec(l, B_DOWN, lanes(n0), nt))).astype(BF16)

        return epi

    seq = 2 * 128
    hg = 4

    def attn_unit():
        lane = lax.broadcasted_iota(jnp.int32, (1, seq), 1)
        gw = hg * hd
        scale = hd ** -0.5

        def window(q2, k2, v2, offs):
            ms = [jnp.logical_and(lane >= o, lane < o + hd).astype(BF16) for o in offs]
            ks = jnp.concatenate([k2 * m for m in ms], axis=0)
            vs = jnp.concatenate([v2 * m for m in ms], axis=0)
            s = lax.dot_general(q2, ks, (((1,), (1,)), ((), ())), preferred_element_type=F32) * scale
            ps = []
            for i in range(len(offs)):
                si = s[:, i * seq:(i + 1) * seq]
                e = jnp.exp(si - jnp.max(si, axis=-1, keepdims=True))
                ps.append((e / jnp.sum(e, axis=-1, keepdims=True)).astype(BF16))
            return jnp.dot(jnp.concatenate(ps, axis=1), vs, preferred_element_type=F32)

        def unit(u):
            img, grp = u // (heads // hg), u % (heads // hg)
            msl = pl.ds(pl.multiple_of(img * seq, seq), seq)

            def win_(base, off):
                return qkv[msl, pl.ds(pl.multiple_of(base * width + grp * gw + off, 128), seq)]

            o0 = window(win_(0, 0), win_(1, 0), win_(2, 0), (0, hd))
            o1 = window(win_(0, 128), win_(1, 128), win_(2, 128), (2 * hd - 128, 3 * hd - 128))
            c0 = grp * gw
            h[msl, pl.ds(pl.multiple_of(c0, 128), 128)] = o0[:, :128].astype(BF16)
            h[msl, pl.ds(pl.multiple_of(c0 + 128, 128), 128)] = (o0[:, 128:] + o1[:, :128]).astype(BF16)
            h[msl, pl.ds(pl.multiple_of(c0 + 256, 128), 128)] = o1[:, 128:].astype(BF16)

        return (rows // seq) * (heads // hg), unit

    def build_vectors():
        wait_bytes(vecg.at[pl.ds(0, nz)], vec_d)
        nd = nz * CORES
        for a in range(nd // 4):
            s = vecg[4 * a].astype(F32)
            for r in range(1, 4):
                s = s + vecg[4 * a + r].astype(F32)
            for l in range(2):
                for k in (LN1_S, LN1_B, B_OUT, LN2_S, LN2_B, B_DOWN):
                    wv = width // (nd // 4)
                    vrow[l * 8 + k:l * 8 + k + 1, a * wv:(a + 1) * wv] = s[l * 8 + k:l * 8 + k + 1, :wv]
                wv = 3 * width // (nd // 4)
                vrow[l * 8 + B_QKV:l * 8 + B_QKV + 1, a * wv:(a + 1) * wv] = s[l * 8 + B_QKV:l * 8 + B_QKV + 1, :wv]
        wv = vrow.shape[1] // nd
        for o in range(nd):
            s = vecg[o].astype(F32)
            for l in range(2):
                vrow[l * 8 + B_UP:l * 8 + B_UP + 1, o * wv:(o + 1) * wv] = s[l * 8 + B_UP:l * 8 + B_UP + 1, :wv]

    last = GROUPS[-1][-1]
    zrows = CORES * win[DOWN].shape[1]
    dq = width // 4

    def slot_copies(t):
        za, zb = (z - t + nz) % nz, (z + t) % nz
        for n, (zz, q, r0, c0) in enumerate(((za, 0, 0, 0), (za, 2, 0, dq), (zb, 1, zrows, 0), (zb, 3, zrows, dq))):
            yield pltpu.make_async_copy(
                gath[DOWN].at[last[0], pl.ds(pl.multiple_of(zz * zrows, 8), zrows), pl.ds(q * dq, dq)],
                wt.at[t % 2, pl.ds(r0, zrows), pl.ds(c0, dq)], tile_sem.at[t % 2])

    def slot_ready(t):
        l, kind = last
        wait_bytes(gath[kind].at[l, pl.ds(0, win[kind].shape[1]), :], rec_l.at[t])
        for cp in slot_copies(t):
            cp.start()

    def slot_wait(t):
        pltpu.make_async_copy(wt.at[t % 2], wt.at[t % 2], tile_sem.at[t % 2]).wait()

    def slot_compute(t):
        za, zb = (z - t + nz) % nz, (z + t) % nz

        def body(mb, carry):
            msl = pl.ds(pl.multiple_of(mb * mrows, mrows), mrows)
            for zz, r0, cols in ((za, 0, (0, 2)), (zb, zrows, (1, 3))):
                res = jnp.dot(g[msl, pl.ds(pl.multiple_of(zz * zrows, 128), zrows)], wt[t % 2, r0:r0 + zrows, :], preferred_element_type=F32)
                for n, q in enumerate(cols):
                    acc[msl, q * dq:(q + 1) * dq] += res[:, n * dq:(n + 1) * dq]
            return carry

        lax.fori_loop(0, mblocks, body, 0)

    vec_mine = vecg.at[f]
    remote(vec_in, vec_mine, snd_v.at[0], vec_a.at[0], up_dev).start()
    remote(vec_in, vec_mine, snd_v.at[1], vec_b.at[0], dn_dev).start()
    remote(vec_in, vec_mine, snd_v.at[2], vec_d, sib_dev).start()
    for j in range(SUB):
        own_send(0, j)
    own_d2d(0)
    load_x = pltpu.make_async_copy(x_in, x, out_sem.at[0])
    load_x.start()
    load_v = pltpu.make_async_copy(vec_in, vec_mine, out_sem.at[1])
    load_v.start()
    for l in range(2):
        for kind in range(4):
            pltpu.make_async_copy(win[kind].at[l], bounce[kind], loc.at[kind]).start()
        for kind in range(4):
            r = shard_rows(kind)
            pltpu.make_async_copy(win[kind].at[l], bounce[kind], loc.at[kind]).wait()
            pltpu.make_async_copy(bounce[kind], gath[kind].at[l, pl.ds(pl.multiple_of(f * r, 8), r), :], loc.at[kind]).start()
        for kind in range(4):
            r = shard_rows(kind)
            pltpu.make_async_copy(bounce[kind], gath[kind].at[l, pl.ds(pl.multiple_of(f * r, 8), r), :], loc.at[kind]).wait()
    load_x.wait()
    load_v.wait()

    def start_group(grp):
        own_d2d(grp)
        run(grp, 0, SUB)
        run(grp, SUB, SUB + 2)
        await_group(grp - 1)

    qkv0_n, qkv0_u, qkv0_s = mm_unit((0, QKV), h, qkv_epi(0))
    out0_n, out0_u, out0_s = mm_unit((0, OUT), h, out_epi(0))
    up0_n, up0_u, up0_s = mm_unit((0, UP), h, up_epi(0))
    down0_n, down0_u, down0_s = mm_unit((0, DOWN), g, down_epi(0, gath[DOWN].shape[1] // kt))
    qkv1_n, qkv1_u, qkv1_s = mm_unit((1, QKV), h, qkv_epi(1))
    out1_n, out1_u, out1_s = mm_unit((1, OUT), h, out_epi(1))
    up1_n, up1_u, up1_s = mm_unit((1, UP), h, up_epi(1))
    at_n, at_u = attn_unit()

    run(0, 0, SUB)
    run(0, SUB, 13)
    build_vectors()
    run(0, 13, ticks, *ln_unit(0, LN1_S, LN1_B))

    def begin(s):
        if COMPUTE:
            s()

    start_group(1)
    begin(qkv0_s)
    run(1, 5, 12, qkv0_n, qkv0_u)
    run(1, 12, ticks, at_n, at_u)

    start_group(2)
    begin(out0_s)
    run(2, 5, 8, out0_n, out0_u)
    begin(up0_s)
    run(2, 8, 9, *ln_unit(0, LN2_S, LN2_B))
    run(2, 9, ticks, up0_n, up0_u)

    start_group(3)
    begin(down0_s)
    run(3, 5, 19, down0_n, down0_u)
    run(3, 19, ticks, *ln_unit(1, LN1_S, LN1_B))

    start_group(4)
    begin(qkv1_s)
    run(4, 5, 11, qkv1_n, qkv1_u)
    run(4, 11, 17, at_n, at_u)
    begin(out1_s)
    run(4, 17, 20, out1_n, out1_u)
    run(4, 20, ticks, *ln_unit(1, LN2_S, LN2_B))

    start_group(5)
    begin(up1_s)
    run(5, 5, 15, up1_n, up1_u)
    acc[...] = jnp.zeros_like(acc)
    slot_ready(0)

    def slots(u):
        slot_wait(u)
        slot_ready(u + 1)
        slot_compute(u)

    if not COMPUTE:
        slot_wait(0)
    run(5, 15, ticks, steps - 1, slots)
    if COMPUTE:
        for j in range(SUB):
            xy_arrive(5, steps, j)
            if j == 0:
                slot_wait(steps - 1)
                slot_compute(steps - 1)
        slot_ready(steps)
        slot_wait(steps)
        slot_compute(steps)
    else:
        for j in range(SUB):
            xy_arrive(5, steps, j)
        for t in range(1, steps + 1):
            slot_ready(t)
            slot_wait(t)
    for mb in range(mblocks):
        msl = pl.ds(mb * mrows, mrows)
        x[msl, :] = (x[msl, :].astype(F32) + (acc[msl, :] + vec(1, B_DOWN, 0, width))).astype(BF16)
        pltpu.make_async_copy(x.at[msl], out_ref.at[msl], out_sem.at[mb]).start()
    for w in [w for grp in GROUPS for w in grp]:
        for sem in (snd_a, snd_b, snd_x, snd_y):
            wait_bytes(amount(w, steps), sem.at[wid(w)])
        wait_bytes(amount(w, 4 * nz), snd_d.at[wid(w)])
    wait_bytes(vecg.at[pl.ds(0, nz // 2)], snd_v.at[0])
    wait_bytes(vecg.at[pl.ds(0, nz // 2 - 1)], snd_v.at[1])
    wait_bytes(vecg.at[pl.ds(0, nz)], snd_v.at[2])
    for mb in range(mblocks):
        msl = pl.ds(mb * mrows, mrows)
        pltpu.make_async_copy(x.at[msl], out_ref.at[msl], out_sem.at[mb]).wait()


def solution(mesh):
    batch_spec = P(('dp', 'fsdp'), None, None)
    vector_spec = P(None, 'fsdp')
    matrix_spec = P(None, 'fsdp', None)
    in_specs = (batch_spec, vector_spec, vector_spec, P(None, 'fsdp', None, None, None), vector_spec, matrix_spec, vector_spec,
                vector_spec, vector_spec, matrix_spec, vector_spec, matrix_spec, vector_spec)
    nd = mesh.shape['fsdp']
    nz = nd // CORES
    ny = math.isqrt(mesh.shape['dp'])

    def local(images, ln1_s, ln1_b, w_qkv, b_qkv, w_out, b_out, ln2_s, ln2_b, w_up, b_up, w_down, b_down):
        nimg, seq, width = images.shape
        layers = w_qkv.shape[0]
        heads, hd = w_qkv.shape[3], w_qkv.shape[4]
        rows = nimg * seq
        x = images.reshape(rows, width)
        wq = w_qkv.reshape(layers, w_qkv.shape[1], 3 * width)
        vw = 4 * b_qkv.shape[1]
        pos = lax.rem(lax.axis_index('fsdp'), 4)
        lane = jnp.arange(vw)

        def place(v):
            n = v.shape[1]
            return jnp.where(lane // n == pos, jnp.tile(v, (1, vw // n)), jnp.zeros((), v.dtype))

        plain = jnp.pad(b_up, ((0, 0), (0, vw - b_up.shape[1])))
        vecs = jnp.stack([place(ln1_s), place(ln1_b), place(b_qkv), place(b_out), place(ln2_s), place(ln2_b), plain, place(b_down)], axis=1)
        vecs = vecs.reshape(layers * 8, vw)
        mats = (wq, w_out, w_up, w_down)
        any_spec = pl.BlockSpec(memory_space=pl.ANY)
        dma = pltpu.SemaphoreType.DMA
        nw = 4 * layers
        gshapes = [jax.ShapeDtypeStruct((layers, nd * m.shape[1], m.shape[2]), BF16) for m in mats]
        outs = pl.pallas_call(
            functools.partial(_kernel, (ny, nz, heads, hd)),
            out_shape=[jax.ShapeDtypeStruct((rows, width), BF16)] + gshapes,
            in_specs=[any_spec] * 6,
            out_specs=[any_spec] * 5,
            scratch_shapes=[
                pltpu.VMEM((rows, width), BF16),
                pltpu.VMEM((rows, width), BF16),
                pltpu.VMEM((rows, 3 * width), BF16),
                pltpu.VMEM((rows, w_up.shape[2]), BF16),
                pltpu.VMEM((rows, width), F32),
                pltpu.VMEM((2, width, width // 2), BF16),
                *[pltpu.VMEM(m.shape[1:], BF16) for m in mats],
                pltpu.VMEM((nd, layers * 8, vw), BF16),
                pltpu.VMEM((layers * 8, w_up.shape[2]), F32),
                *[dma((nw, nz - 1, SUB))] * 4,
                dma((nw,)),
                dma((nz,)),
                *[dma((nw,))] * 5,
                dma((3,)),
                dma((nz // 2,)),
                dma((nz // 2,)),
                dma,
                dma((4,)),
                dma((2,)),
                dma((3,)),
            ],
            compiler_params=pltpu.CompilerParams(collective_id=0, has_side_effects=True, vmem_limit_bytes=60 * 1024 * 1024),
        )(x, vecs, *mats)
        return outs[0].reshape(nimg, seq, width)

    return jax.shard_map(local, mesh=mesh, in_specs=in_specs, out_specs=batch_spec, check_vma=False)
```

time: 745 us -> 333 us (0.45); the launches traced: 737 us -> 333 us
  Pallas kernels: 0 us -> 318 us
  waiting for transfers between devices: 295 us -> 0 us
  matrix products: 257 us -> 0 us
  blocking collectives: 91.6 us -> 0 us
  local copies, waits for them, and re-layouts: 70.7 us -> 14.8 us
  between operations: 15.7 us -> 0.05 us
    pallas_call x0 -> x1, Pallas kernels: none -> 318 us  [local(): pl.pallas_call(functools.partial(_kernel, (ny, nz, heads, hd)), out_shape...]
    all_gather x8 -> x0, waiting for transfers between devices: 292 us -> none  [fetch(): return lax.all_gather(stored[name][layer], 'fsdp', axis=0, tiled=True)]
    dot_general x40 -> x0, matrix products: 212 us -> none  [the longest x32 73.3 us: one_head(): jnp.einsum('crl,clf->crf', attn_probs, v_head, preferred_element_type=jnp...]
    unnamed x1 -> x0, blocking collectives: 56.3 us -> none
    all_gather x2 -> x0, local copies, waits for them, and re-layouts: 46.4 us -> none  [fetch(): return lax.all_gather(stored[name][layer], 'fsdp', axis=0, tiled=True)]
    sub x32 -> x0, matrix products: 45.5 us -> none  [one_head(): attn_probs = jax.nn.softmax(scores, axis=-1).astype(jnp.bfloat16)]
    all_gather x2 -> x0, blocking collectives: 35.3 us -> none  [fetch(): return lax.all_gather(stored[name][layer], 'fsdp', axis=0, tiled=True)]
  transfers between devices with their start and end apart: 8 -> 0, of which waited for: 5 -> 0; matrix products, arithmetic and copies ran while one was open for 42% -> 0% of each run, Pallas kernels for 0% -> 0%
where the time goes in v1:
time: 333 us
  Pallas kernels  318 us (95%)
  local copies, waits for them, and re-layouts  14.8 us (4%)
    pallas_call x1, Pallas kernels, local(): pl.pallas_call(functools.partial(_kernel, (ny, nz, heads, hd)), out_shape...  318 us

profile of v1, /device:TPU:21, one launch (start us, length us, event | category | flops | bytes accessed | tf_op | source)
XLA Modules:
  0.0 332.7 jit_solution(14523762037242860833)
XLA Ops:
  0.0 0.7 tile.32
  0.7 0.1 tile.33
  0.8 0.7 tile.28
  1.5 0.1 tile.29
  1.6 0.7 tile.30
  2.2 0.1 tile.31
  2.3 0.7 tile.34
  3.0 0.1 tile.70
  3.1 0.7 tile.71
  3.7 0.1 tile.72
  3.8 0.7 tile.73
  4.5 0.1 tile.74
  4.6 0.7 tile.75
  5.2 0.1 tile.76
  5.5 0.7 constant_dynamic-update-slice_fusion.1
  6.2 0.6 copy.17
  6.8 4.9 %reshape.238.refs_0_ = bf16[2,96,4608]{2,1,0:T(8,128)(2,1)} reshape(bf16[2,96,3,16,96]{4,3,2,1,0:T(8,128)(2,1)} %param.16) | data formatting | bytes 3538944 | tf_op jit(solution)/shard_map/reshape | solution.py:490
  11.7 317.8 %shard_map.127 = (bf16[768,1536]{1,0:T(8,128)(2,1)}, bf16[2,1536,4608]{2,1,0:T(8,128)(2,1)}, bf16[2,1536,1536]{2,1,0:T(8,128)(2,1)}, bf16[2,1536,6144]{2,1,0:T(8,128)(2,1)}, bf16[2,6144,1536]{2,1,0:T(8,128)(2,1)}) custom-call(bf16[768,1536]{1,0:T(8,128)(2,1)} %bitcast.10, bf16[16,1152]{1,0:T(8,128)(2,1)} %bitcast.11, bf16[2,96,4608]{2,1,0:T(8,128)(2,1)} %reshape.238.refs_0_, ...), custom_call_target="tpu_custom_call" | custom-call | tf_op jit(solution)/shard_map/pallas_call | solution.py:507
  329.5 3.2 copy.26
  (8 shorter events, 0.1 us)

commit v2 on v1

v2 whole, which is shorter than its diff:
```python
import functools
import math

import jax
import jax.numpy as jnp
from jax import lax
from jax.experimental import pallas as pl
from jax.experimental.pallas import tpu as pltpu
from jax.sharding import PartitionSpec as P

LN_EPS = 1e-6
GELU_C = math.sqrt(2.0 / math.pi)
MESH = pl.DeviceIdType.MESH
CORES = 2
SUB = 3
COMPUTE = True

LN1_S, LN1_B, B_QKV, B_OUT, LN2_S, LN2_B, B_UP, B_DOWN = range(8)
QKV, OUT, UP, DOWN = range(4)
GROUPS = (((0, QKV), (0, OUT)), ((0, UP),), ((0, DOWN),), ((1, QKV), (1, OUT)), ((1, UP),), ((1, DOWN),))
F32 = jnp.float32
BF16 = jnp.bfloat16


def _pack(ins, out):
    pos = lax.rem(lax.axis_index('fsdp'), 4)
    out[...] = jnp.zeros_like(out)
    for k, ref in enumerate(ins):
        n = ref.shape[1]
        if k == B_UP:
            out[2 * k:2 * k + 2, :n] = ref[...]
            continue
        src = lax.broadcasted_iota(jnp.int32, (n, 4 * n), 0)
        dst = lax.broadcasted_iota(jnp.int32, (n, 4 * n), 1)
        pick = (dst == src + pos * n).astype(BF16)
        out[2 * k:2 * k + 2, :4 * n] = jnp.dot(ref[...], pick, preferred_element_type=F32).astype(BF16)


def _kernel(dims, x_in, *refs):
    ny, nz, heads, hd = dims
    vin, win, refs = refs[:8], refs[8:12], refs[12:]
    out_ref, vec_in, refs = refs[0], refs[1], refs[2:]
    gath, refs = refs[:4], refs[4:]
    x, h, qkv, g, acc, wt, wl = refs[:7]
    bounce, refs = refs[7:11], refs[11:]
    vecg, vrow, vown, raw, raw32 = refs[:5]
    (rec_a, rec_b, rec_x, rec_y, rec_d, rec_l, snd_a, snd_b, snd_x, snd_y, snd_d, snd_v, vec_a, vec_b, vec_d, loc, tile_sem,
     out_sem) = refs[5:]

    rows, width = x.shape
    mblocks = 3
    mrows = rows // mblocks
    steps = nz - 1
    ticks = steps * SUB

    d = lax.axis_index('dp')
    f = lax.axis_index('fsdp')
    z, c = f // CORES, f % CORES
    up_dev = (d, ((z + 1) % nz) * CORES + c)
    dn_dev = (d, ((z + nz - 1) % nz) * CORES + c)
    sib_dev = (d, z * CORES + (CORES - 1 - c))
    x_dev = (d + ny * (1 - 2 * ((d // ny) % 2)), f)
    y_dev = (d + 1 - 2 * (d % 2), f)
    par = (d // ny + d % ny) % 2
    qa, qb = 2 * par, 2 * par + 1
    qx, qy = 2 * (1 - par), 2 * (1 - par) + 1

    def remote(src, dst, ssem, rsem, dev):
        return pltpu.make_async_remote_copy(src_ref=src, dst_ref=dst, send_sem=ssem, recv_sem=rsem, device_id=dev,
                                            device_id_type=MESH)

    def wid(w):
        return w[0] * 4 + w[1]

    def shard_rows(kind):
        return win[kind].shape[1]

    def part(ref, w, origin, q, j):
        l, kind = w
        r = shard_rows(kind)
        if kind == DOWN:
            n = r // SUB
            cols = ref.shape[2] // 4
            return ref.at[l, pl.ds(pl.multiple_of(origin * r + j * n, 8), n), pl.ds(pl.multiple_of(q * cols, 128), cols)]
        n = r // (4 * SUB)
        return ref.at[l, pl.ds(pl.multiple_of(origin * r + q * (r // 4) + j * n, 8), n), :]

    def quarter(ref, w, origin, q):
        l, kind = w
        r = shard_rows(kind)
        if kind == DOWN:
            cols = ref.shape[2] // 4
            return ref.at[l, pl.ds(pl.multiple_of(origin * r, 8), r), pl.ds(pl.multiple_of(q * cols, 128), cols)]
        return ref.at[l, pl.ds(pl.multiple_of(origin * r + q * (r // 4), 8), r // 4), :]

    def to_sibling(w, t, origin, q):
        p = quarter(gath[w[1]], w, origin, q)
        remote(p, p, snd_d.at[wid(w)], d2d_sem(w, t), sib_dev).start()

    def amount(w, quarters):
        l, kind = w
        r, cols = shard_rows(kind), gath[kind].shape[2]
        if kind == DOWN and quarters % 4:
            return gath[kind].at[l, pl.ds(0, quarters * r), pl.ds(0, cols // 4)]
        return gath[kind].at[l, pl.ds(0, quarters * (r // 4)), :]

    def wait_bytes(view, sem):
        pltpu.make_async_copy(view, view, sem).wait()

    def d2d_sem(w, t):
        return rec_l.at[t] if w == GROUPS[-1][-1] else rec_d.at[wid(w)]

    def own_send(grp, j, kinds=(QKV, OUT, UP, DOWN)):
        for w in GROUPS[grp]:
            l, kind = w
            if kind not in kinds:
                continue
            for q, snd, rec, dev in ((qa, snd_a, rec_a, up_dev), (qb, snd_b, rec_b, dn_dev)):
                dst = part(gath[kind], w, f, q, j)
                src = dst if kind == QKV else part(win[kind], w, 0, q, j)
                remote(src, dst, snd.at[wid(w)], rec.at[wid(w), 0, j], dev).start()

    def own_d2d(grp):
        for w in GROUPS[grp]:
            l, kind = w
            r = shard_rows(kind)
            dst = gath[kind].at[l, pl.ds(pl.multiple_of(f * r, 8), r), :]
            remote(dst if kind == QKV else win[kind].at[l], dst, snd_d.at[wid(w)], d2d_sem(w, 0), sib_dev).start()

    def xy_arrive(grp, t, j):
        oa = ((z - t + nz) % nz) * CORES + c
        ob = ((z + t) % nz) * CORES + c
        for w in GROUPS[grp]:
            l, kind = w
            px, py = part(gath[kind], w, oa, qx, j), part(gath[kind], w, ob, qy, j)
            remote(px, px, snd_x.at[wid(w)], rec_x.at[wid(w), t - 1, j], x_dev).wait_recv()
            remote(px, px, snd_d.at[wid(w)], d2d_sem(w, t), sib_dev).start()
            remote(py, py, snd_y.at[wid(w)], rec_y.at[wid(w), t - 1, j], y_dev).wait_recv()
            remote(py, py, snd_d.at[wid(w)], d2d_sem(w, t), sib_dev).start()

    def tick(grp, i, early):
        t, j = i // SUB + 1, i % SUB
        oa = ((z - t + nz) % nz) * CORES + c
        ob = ((z + t) % nz) * CORES + c
        for w in GROUPS[grp]:
            l, kind = w
            for o, q, snd, rec, dev in ((oa, qa, snd_a, rec_a, up_dev), (ob, qb, snd_b, rec_b, dn_dev)):
                p = part(gath[kind], w, o, q, j)
                remote(p, p, snd.at[wid(w)], rec.at[wid(w), t - 1, j], dev).wait_recv()

                @pl.when(t < steps)
                def _():
                    remote(p, p, snd.at[wid(w)], rec.at[wid(w), t, j], dev).start()

            pa, pb = part(gath[kind], w, oa, qa, j), part(gath[kind], w, ob, qb, j)
            remote(pa, pa, snd_x.at[wid(w)], rec_x.at[wid(w), t - 1, j], x_dev).start()
            remote(pb, pb, snd_y.at[wid(w)], rec_y.at[wid(w), t - 1, j], y_dev).start()
        if grp + 1 < len(GROUPS):

            @pl.when(t == steps - 1)
            def _():
                own_send(grp + 1, j)

        if grp == 0:
            half = nz // 2
            va, vb = vecg.at[oa], vecg.at[ob]

            @pl.when(jnp.logical_and(j == 0, t <= half))
            def _():
                remote(va, va, snd_v.at[0], vec_a.at[t - 1], up_dev).wait_recv()

                @pl.when(t < half)
                def _():
                    remote(va, va, snd_v.at[0], vec_a.at[t], up_dev).start()

                remote(va, va, snd_v.at[2], vec_d, sib_dev).start()

            @pl.when(jnp.logical_and(j == 0, t < half))
            def _():
                remote(vb, vb, snd_v.at[1], vec_b.at[t - 1], dn_dev).wait_recv()

                @pl.when(t < half - 1)
                def _():
                    remote(vb, vb, snd_v.at[1], vec_b.at[t], dn_dev).start()

                remote(vb, vb, snd_v.at[2], vec_d, sib_dev).start()

        if not early:
            xy_arrive(grp, t - 1, j)
        elif grp > 0:
            xy_arrive(grp - 1, steps, j)

        @pl.when(j == SUB - 1)
        def _():
            for w in GROUPS[grp]:
                to_sibling(w, t, oa, qa)
                to_sibling(w, t, ob, qb)

    def run(grp, lo, hi, total=0, unit=None):
        def body(i, carry):
            tick(grp, i, hi <= SUB)
            if unit is not None and COMPUTE:
                k = i - lo
                lax.fori_loop((k * total) // (hi - lo), ((k + 1) * total) // (hi - lo), lambda u, cc: (unit(u), cc)[1], 0)
            return carry

        lax.fori_loop(lo, hi, body, 0)

    def await_group(grp):
        for w in GROUPS[grp]:
            wait_bytes(amount(w, 4 * nz), rec_d.at[wid(w)])

    def vec(l, k, n, width_):
        return vrow[pl.ds(2 * k + l, 1), pl.ds(n, width_)]

    def ln_unit(l, ks, kb):
        n = 64

        def unit(u):
            sl = pl.ds(pl.multiple_of(u * n, n), n)
            v = x[sl, :].astype(F32)
            v = v - jnp.mean(v, axis=-1, keepdims=True)
            var = jnp.mean(v * v, axis=-1, keepdims=True)
            y = v * lax.rsqrt(var + LN_EPS)
            h[sl, :] = (y * vec(l, ks, 0, width) + vec(l, kb, 0, width)).astype(BF16)

        return rows // n, unit

    kt, nt = wt.shape[1], wt.shape[2]
    nu = nt // 2

    def tile_copies(w, i):
        l, kind = w
        ref, dst, sem = gath[kind].at[l], wt.at[i % 2], tile_sem.at[i % 2]
        if kind != DOWN:
            return [pltpu.make_async_copy(ref.at[:, pl.ds(pl.multiple_of(i * nt, 128), nt)], dst, sem)]
        n, k = i // 2, i % 2
        return [
            pltpu.make_async_copy(
                ref.at[pl.ds(pl.multiple_of((2 * k + s) * kt, 8), kt), pl.ds(pl.multiple_of(n * nu, 128), nu)],
                dst.at[:, pl.ds(s * nu, nu)], sem) for s in range(2)
        ]

    def tile_start(w, i):
        for cp in tile_copies(w, i):
            cp.start()

    def tile_wait(i):
        pltpu.make_async_copy(wt.at[i % 2], wt.at[i % 2], tile_sem.at[i % 2]).wait()

    def mm_unit(w, a_ref, epilogue):
        l, kind = w
        ntiles = gath[kind].shape[2] // nt if kind != DOWN else 2 * (gath[kind].shape[2] // nu)

        def unit(i):
            tile_wait(i)

            @pl.when(i + 1 < ntiles)
            def _():
                tile_start(w, i + 1)

            if kind == DOWN:
                n, k = i // 2, i % 2
                n0 = pl.multiple_of(n * nu, 128)
                res = sum(
                    jnp.dot(a_ref[:, pl.ds(pl.multiple_of((2 * k + s) * kt, 128), kt)], wt[i % 2, :, s * nu:(s + 1) * nu],
                            preferred_element_type=F32) for s in range(2))
                epilogue(res, pl.ds(n0, nu), n0, k)
                return
            for s in range(nt // nu):
                n0 = pl.multiple_of(i * nt + s * nu, 128)
                res = jnp.dot(a_ref[...], wt[i % 2, :, s * nu:(s + 1) * nu], preferred_element_type=F32)
                epilogue(res, pl.ds(n0, nu), n0, 0)

        return ntiles, unit, lambda: tile_start(w, 0)

    def gelu_tanh(v):
        half = 0.5 * v
        return half + half * jnp.tanh(v * (GELU_C + (GELU_C * 0.044715) * (v * v)))

    def qkv_epi(l):
        def epi(res, nsl, n0, k):
            qkv[:, nsl] = (res + vec(l, B_QKV, n0, nu)).astype(BF16)

        return epi

    def out_epi(l):
        def epi(res, nsl, n0, k):
            x[:, nsl] = (x[:, nsl].astype(F32) + (res + vec(l, B_OUT, n0, nu))).astype(BF16)

        return epi

    def up_epi(l):
        def epi(res, nsl, n0, k):
            g[:, nsl] = gelu_tanh(res + vec(l, B_UP, n0, nu)).astype(BF16)

        return epi

    def down_epi(l):
        def epi(res, nsl, n0, k):
            @pl.when(k == 0)
            def _():
                acc[:, nsl] = res

            @pl.when(k == 1)
            def _():
                x[:, nsl] = (x[:, nsl].astype(F32) + (acc[:, nsl] + res + vec(l, B_DOWN, n0, nu))).astype(BF16)

        return epi

    seq = 2 * 128
    hg = 4

    def attn_unit():
        lane = lax.broadcasted_iota(jnp.int32, (1, seq), 1)
        gw = hg * hd
        scale = hd ** -0.5 * math.log2(math.e)

        def window(q2, k2, v2, offs):
            ms = [jnp.logical_and(lane >= o, lane < o + hd).astype(BF16) for o in offs]
            ks = jnp.concatenate([k2 * m for m in ms], axis=0)
            vs = jnp.concatenate([v2 * m for m in ms], axis=0)
            s = lax.dot_general(q2, ks, (((1,), (1,)), ((), ())), preferred_element_type=F32)
            ps = []
            for i in range(len(offs)):
                si = s[:, i * seq:(i + 1) * seq]
                e = jnp.exp2((si - jnp.max(si, axis=-1, keepdims=True)) * scale)
                ps.append((e * (1.0 / jnp.sum(e, axis=-1, keepdims=True))).astype(BF16))
            return jnp.dot(jnp.concatenate(ps, axis=1), vs, preferred_element_type=F32)

        def unit(u):
            img, grp = u // (heads // hg), u % (heads // hg)
            msl = pl.ds(pl.multiple_of(img * seq, seq), seq)

            def win_(base, off):
                return qkv[msl, pl.ds(pl.multiple_of(base * width + grp * gw + off, 128), seq)]

            o0 = window(win_(0, 0), win_(1, 0), win_(2, 0), (0, hd))
            o1 = window(win_(0, 128), win_(1, 128), win_(2, 128), (2 * hd - 128, 3 * hd - 128))
            c0 = grp * gw
            h[msl, pl.ds(pl.multiple_of(c0, 128), 128)] = o0[:, :128].astype(BF16)
            h[msl, pl.ds(pl.multiple_of(c0 + 128, 128), 128)] = (o0[:, 128:] + o1[:, :128]).astype(BF16)
            h[msl, pl.ds(pl.multiple_of(c0 + 256, 128), 128)] = o1[:, 128:].astype(BF16)

        return (rows // seq) * (heads // hg), unit

    def build_vectors():
        wait_bytes(vecg.at[pl.ds(0, nz)], vec_d)
        nd = nz * CORES
        for a in range(nd // 4):
            s = vecg[4 * a].astype(F32)
            for r in range(1, 4):
                s = s + vecg[4 * a + r].astype(F32)
            for l in range(2):
                for k in (LN1_S, LN1_B, B_OUT, LN2_S, LN2_B, B_DOWN):
                    wv = width // (nd // 4)
                    vrow[2 * k + l:2 * k + l + 1, a * wv:(a + 1) * wv] = s[2 * k + l:2 * k + l + 1, :wv]
                wv = 3 * width // (nd // 4)
                vrow[2 * B_QKV + l:2 * B_QKV + l + 1, a * wv:(a + 1) * wv] = s[2 * B_QKV + l:2 * B_QKV + l + 1, :wv]
        wv = vrow.shape[1] // nd
        for o in range(nd):
            s = vecg[o].astype(F32)
            for l in range(2):
                vrow[2 * B_UP + l:2 * B_UP + l + 1, o * wv:(o + 1) * wv] = s[2 * B_UP + l:2 * B_UP + l + 1, :wv]

    last = GROUPS[-1][-1]
    zrows = CORES * win[DOWN].shape[1]
    dq = width // 4

    def slot_copies(t):
        za, zb = (z - t + nz) % nz, (z + t) % nz
        for n, (zz, q, r0, c0) in enumerate(((za, 0, 0, 0), (za, 2, 0, dq), (zb, 1, zrows, 0), (zb, 3, zrows, dq))):
            yield pltpu.make_async_copy(
                gath[DOWN].at[last[0], pl.ds(pl.multiple_of(zz * zrows, 8), zrows), pl.ds(q * dq, dq)],
                wl.at[t % 2, pl.ds(r0, zrows), pl.ds(c0, dq)], tile_sem.at[t % 2])

    def slot_ready(t):
        l, kind = last
        wait_bytes(gath[kind].at[l, pl.ds(0, win[kind].shape[1]), :], rec_l.at[t])
        for cp in slot_copies(t):
            cp.start()

    def slot_wait(t):
        pltpu.make_async_copy(wl.at[t % 2], wl.at[t % 2], tile_sem.at[t % 2]).wait()

    def slot_compute(t):
        za, zb = (z - t + nz) % nz, (z + t) % nz

        for zz, r0, c0 in ((za, 0, 0), (zb, zrows, 2 * dq)):
            for nn in range(2 * dq // nu):
                csl = slice(c0 + nn * nu, c0 + (nn + 1) * nu)
                acc[:, csl] += jnp.dot(g[:, pl.ds(pl.multiple_of(zz * zrows, 128), zrows)],
                                       wl[t % 2, r0:r0 + zrows, nn * nu:(nn + 1) * nu], preferred_element_type=F32)

    vec_mine = vecg.at[f]
    load_x = pltpu.make_async_copy(x_in, x, out_sem.at[0])
    load_v = pltpu.make_async_copy(vec_in, vec_mine, out_sem.at[1])

    def own_load(kind):
        return pltpu.make_async_copy(win[kind], bounce[kind], loc.at[kind])

    def own_store(l, kind):
        r = shard_rows(kind)
        return pltpu.make_async_copy(bounce[kind].at[l], gath[kind].at[l, pl.ds(pl.multiple_of(f * r, 8), r), :], loc.at[4 * (l + 1) + kind])

    def load_raw(l):
        return pltpu.make_async_copy(win[QKV].at[l], raw, loc.at[QKV])

    def relayout(l, first, r):
        nh = raw.shape[1]
        wide, groups = r // 8, nh // hg

        def unit(u):
            @pl.when(u < wide)
            def _():
                raw32[pl.ds(pl.multiple_of(u * 8 * nh, 8), 8 * nh), :] = raw[pl.ds(pl.multiple_of(first + u * 8, 8), 8)].astype(F32).reshape(8 * nh, hd)

            @pl.when(u >= wide)
            def _():
                i = u - wide
                src = lax.broadcasted_iota(jnp.int32, (hd, hg * hd), 0)
                dst = lax.broadcasted_iota(jnp.int32, (hd, hg * hd), 1)
                res = sum(
                    jnp.dot(raw32[pl.ds(hg * i + k, r, stride=nh), :].astype(BF16), (dst == src + k * hd).astype(BF16),
                            preferred_element_type=F32) for k in range(hg))
                bounce[QKV][l, pl.ds(pl.multiple_of(first, 8), r), pl.ds(pl.multiple_of(i * hg * hd, 128), hg * hd)] = res.astype(BF16)

        return wide + groups, unit

    load_raw(0).start()
    load_x.start()
    for kind in (OUT, UP, DOWN):
        own_load(kind).start()
    barrier = pltpu.get_barrier_semaphore()
    for dev in (up_dev, dn_dev, sib_dev, x_dev, y_dev):
        pl.semaphore_signal(barrier, inc=1, device_id=dev, device_id_type=MESH)
    half_rows = raw.shape[0] // 2
    mine, other = par * half_rows, (1 - par) * half_rows

    def half_store(first):
        r = shard_rows(QKV)
        return pltpu.make_async_copy(bounce[QKV].at[0, pl.ds(pl.multiple_of(first, 8), half_rows)],
                                     gath[QKV].at[0, pl.ds(pl.multiple_of(f * r + first, 8), half_rows), :], loc.at[4 + QKV])

    def relay_half(first):
        n_re, re0 = relayout(0, first, half_rows)
        lax.fori_loop(0, n_re, lambda u, cc: (re0(u), cc)[1], 0)
        half_store(first).start()

    pl.semaphore_wait(barrier, 5)
    for j in range(SUB):
        own_send(0, j, (OUT,))
    load_raw(0).wait()
    relay_half(mine)
    _pack(vin, vown)
    save_v = pltpu.make_async_copy(vown, vec_in, out_sem.at[1])
    save_v.start()
    half_store(mine).wait()
    for j in range(SUB):
        own_send(0, j, (QKV,))
    save_v.wait()
    remote(vec_in, vec_mine, snd_v.at[0], vec_a.at[0], up_dev).start()
    remote(vec_in, vec_mine, snd_v.at[1], vec_b.at[0], dn_dev).start()
    load_v.start()
    relay_half(other)
    load_raw(1).start()
    half_store(other).wait()
    remote(vec_in, vec_mine, snd_v.at[2], vec_d, sib_dev).start()
    own_d2d(0)
    for kind in (OUT, UP, DOWN):
        own_load(kind).wait()
        for l in range(2):
            own_store(l, kind).start()

    def start_group(grp, first=(), second=()):
        run(grp, 0, SUB, *first)
        run(grp, SUB, SUB + 1, *second)
        await_group(grp - 1)
        own_d2d(grp)

    qkv0_n, qkv0_u, qkv0_s = mm_unit((0, QKV), h, qkv_epi(0))
    out0_n, out0_u, out0_s = mm_unit((0, OUT), h, out_epi(0))
    up0_n, up0_u, up0_s = mm_unit((0, UP), h, up_epi(0))
    down0_n, down0_u, down0_s = mm_unit((0, DOWN), g, down_epi(0))
    qkv1_n, qkv1_u, qkv1_s = mm_unit((1, QKV), h, qkv_epi(1))
    out1_n, out1_u, out1_s = mm_unit((1, OUT), h, out_epi(1))
    up1_n, up1_u, up1_s = mm_unit((1, UP), h, up_epi(1))
    at_n, at_u = attn_unit()

    def begin(s):
        if COMPUTE:
            s()

    run(0, 0, SUB)
    load_raw(1).wait()
    run(0, SUB, 13, *relayout(1, 0, raw.shape[0]))
    own_store(1, QKV).start()
    run(0, 13, 14)
    load_v.wait()
    load_x.wait()
    for kind in range(4):
        for l in range(2):
            if (l, kind) != (0, QKV):
                own_store(l, kind).wait()
    build_vectors()
    run(0, 14, ticks, *ln_unit(0, LN1_S, LN1_B))

    start_group(1)
    begin(qkv0_s)
    run(1, 4, 13, qkv0_n, qkv0_u)
    run(1, 13, ticks, at_n, at_u)

    begin(out0_s)
    start_group(2, (2, out0_u), (out0_n - 2, lambda u: out0_u(u + 2)))
    begin(up0_s)
    run(2, 4, 7, *ln_unit(0, LN2_S, LN2_B))
    run(2, 7, ticks, up0_n, up0_u)

    start_group(3)
    begin(down0_s)
    run(3, 4, 17, down0_n, down0_u)
    run(3, 17, ticks, *ln_unit(1, LN1_S, LN1_B))
    acc[...] = jnp.zeros_like(acc)

    start_group(4)
    begin(qkv1_s)
    run(4, 4, 11, qkv1_n, qkv1_u)
    run(4, 11, 16, at_n, at_u)
    begin(out1_s)
    run(4, 16, 19, out1_n, out1_u)
    run(4, 19, ticks, *ln_unit(1, LN2_S, LN2_B))

    start_group(5)
    begin(up1_s)
    run(5, 4, 15, up1_n, up1_u)
    slot_ready(0)

    def slots(u):
        slot_wait(u)
        slot_ready(u + 1)
        slot_compute(u)

    if not COMPUTE:
        slot_wait(0)
    run(5, 15, ticks, steps - 1, slots)
    if COMPUTE:
        for j in range(SUB):
            xy_arrive(5, steps, j)
            if j == 0:
                slot_wait(steps - 1)
                slot_compute(steps - 1)
        slot_ready(steps)
        slot_wait(steps)
        slot_compute(steps)
    else:
        for j in range(SUB):
            xy_arrive(5, steps, j)
        for t in range(1, steps + 1):
            slot_ready(t)
            slot_wait(t)
    for mb in range(mblocks):
        msl = pl.ds(mb * mrows, mrows)
        for n, q in enumerate((0, 2, 1, 3)):
            csl = slice(q * dq, (q + 1) * dq)
            x[msl, csl] = (x[msl, csl].astype(F32) + (acc[msl, n * dq:(n + 1) * dq] + vec(1, B_DOWN, q * dq, dq))).astype(BF16)
        pltpu.make_async_copy(x.at[msl], out_ref.at[msl], out_sem.at[mb]).start()
    for w in [w for grp in GROUPS for w in grp]:
        for sem in (snd_a, snd_b, snd_x, snd_y):
            wait_bytes(amount(w, steps), sem.at[wid(w)])
        wait_bytes(amount(w, 4 * nz), snd_d.at[wid(w)])
    wait_bytes(vecg.at[pl.ds(0, nz // 2)], snd_v.at[0])
    wait_bytes(vecg.at[pl.ds(0, nz // 2 - 1)], snd_v.at[1])
    wait_bytes(vecg.at[pl.ds(0, nz)], snd_v.at[2])
    for mb in range(mblocks):
        msl = pl.ds(mb * mrows, mrows)
        pltpu.make_async_copy(x.at[msl], out_ref.at[msl], out_sem.at[mb]).wait()


def solution(mesh):
    batch_spec = P(('dp', 'fsdp'), None, None)
    vector_spec = P(None, 'fsdp')
    matrix_spec = P(None, 'fsdp', None)
    in_specs = (batch_spec, vector_spec, vector_spec, P(None, 'fsdp', None, None, None), vector_spec, matrix_spec, vector_spec,
                vector_spec, vector_spec, matrix_spec, vector_spec, matrix_spec, vector_spec)
    nd = mesh.shape['fsdp']
    nz = nd // CORES
    ny = math.isqrt(mesh.shape['dp'])

    def local(images, ln1_s, ln1_b, w_qkv, b_qkv, w_out, b_out, ln2_s, ln2_b, w_up, b_up, w_down, b_down):
        nimg, seq, width = images.shape
        layers = w_qkv.shape[0]
        heads, hd = w_qkv.shape[3], w_qkv.shape[4]
        rows = nimg * seq
        x = images.reshape(rows, width)
        vw = 4 * b_qkv.shape[1]
        vecs = (ln1_s, ln1_b, b_qkv, b_out, ln2_s, ln2_b, b_up, b_down)
        mats = (w_qkv.reshape(layers, w_qkv.shape[1], 3 * heads, hd), w_out, w_up, w_down)
        cols = (3 * width, width, w_up.shape[2], width)
        any_spec = pl.BlockSpec(memory_space=pl.ANY)
        dma = pltpu.SemaphoreType.DMA
        nw = 4 * layers
        gshapes = [jax.ShapeDtypeStruct((layers, nd * m.shape[1], n), BF16) for m, n in zip(mats, cols)]
        outs = pl.pallas_call(
            functools.partial(_kernel, (ny, nz, heads, hd)),
            out_shape=[jax.ShapeDtypeStruct((rows, width), BF16), jax.ShapeDtypeStruct((layers * 8, vw), BF16)] + gshapes,
            in_specs=[any_spec] + [pl.BlockSpec(memory_space=pltpu.VMEM)] * 8 + [any_spec] * 4,
            out_specs=[any_spec] * 6,
            scratch_shapes=[
                pltpu.VMEM((rows, width), BF16),
                pltpu.VMEM((rows, width), BF16),
                pltpu.VMEM((rows, 3 * width), BF16),
                pltpu.VMEM((rows, w_up.shape[2]), BF16),
                pltpu.VMEM((rows, width), F32),
                pltpu.VMEM((2, width, width // 3), BF16),
                pltpu.VMEM((2, width, width // 2), BF16),
                *[pltpu.VMEM((*m.shape[:2], n), BF16) for m, n in zip(mats, cols)],
                pltpu.VMEM((nd, layers * 8, vw), BF16),
                pltpu.VMEM((layers * 8, w_up.shape[2]), F32),
                pltpu.VMEM((layers * 8, vw), BF16),
                pltpu.VMEM(mats[0].shape[1:], BF16),
                pltpu.VMEM((mats[0].shape[1] * 3 * heads, hd), F32),
                *[dma((nw, nz - 1, SUB))] * 4,
                dma((nw,)),
                dma((nz,)),
                *[dma((nw,))] * 5,
                dma((3,)),
                dma((nz // 2,)),
                dma((nz // 2,)),
                dma,
                dma((4 * (layers + 1),)),
                dma((2,)),
                dma((3,)),
            ],
            compiler_params=pltpu.CompilerParams(collective_id=0, has_side_effects=True, vmem_limit_bytes=56 * 1024 * 1024),
        )(x, *vecs, *mats)
        return outs[0].reshape(nimg, seq, width)

    return jax.shard_map(local, mesh=mesh, in_specs=in_specs, out_specs=batch_spec, check_vma=False)
```

time: 333 us -> 315 us (0.946)
  local copies, waits for them, and re-layouts: 14.8 us -> 3.22 us
  Pallas kernels: 318 us -> 312 us
    another operation x15 -> x0, local copies, waits for them, and re-layouts: 5.93 us -> none  [the longest x14 5.31 us: place(): jnp.tile(v, (1, vw // n))]
    pallas_call x1, Pallas kernels: 318 us -> 312 us  [local(): pl.pallas_call(functools.partial(_kernel, (ny, nz, heads, hd)), out_shape...]
    reshape x1 -> x0, local copies, waits for them, and re-layouts: 4.93 us -> none  [local(): wq = w_qkv.reshape(layers, w_qkv.shape[1], 3 * width)]
where the time goes in v2:
time: 315 us
  Pallas kernels  312 us (99%)
  local copies, waits for them, and re-layouts  3.22 us (1%)
    pallas_call x1, Pallas kernels, local(): pl.pallas_call(functools.partial(_kernel, (ny, nz, heads, hd)), out_shape...  312 us

profile of v2, /device:TPU:21, one launch (start us, length us, event | category | flops | bytes accessed | tf_op | source)
XLA Modules:
  0.0 315.1 jit_solution(18395990033830236843)
XLA Ops:
  0.0 311.9 %shard_map.127 = (bf16[768,1536]{1,0:T(8,128)(2,1)}, bf16[16,1152]{1,0:T(8,128)(2,1)}, bf16[2,1536,4608]{2,1,0:T(8,128)(2,1)}, bf16[2,1536,1536]{2,1,0:T(8,128)(...) custom-call(bf16[768,1536]{1,0:T(8,128)(2,1)} %bitcast.3, bf16[2,96]{1,0:T(2,128)(2,1)} %refs_0_.1, ...), custom_call_target="tpu_custom_call" | custom-call | tf_op jit(solution)/shard_map/pallas_call | solution.py:603
  311.9 3.2 %copy.15 = bf16[3,256,1536]{2,1,0:T(8,128)(2,1)} copy(bf16[3,256,1536]{2,1,0:T(8,128)(2,1)} %bitcast.5) | data formatting | bytes 4718592

commit v3 on v2

--- a/solution.py
+++ b/solution.py
@@ -9,6 +9,7 @@
 from jax.sharding import PartitionSpec as P
 
 LN_EPS = 1e-6
+COPIES = 8
 GELU_C = math.sqrt(2.0 / math.pi)
 MESH = pl.DeviceIdType.MESH
 CORES = 2
@@ -16,6 +17,7 @@
 COMPUTE = True
 
 LN1_S, LN1_B, B_QKV, B_OUT, LN2_S, LN2_B, B_UP, B_DOWN = range(8)
+SEG_ROWS = 14
 QKV, OUT, UP, DOWN = range(4)
 GROUPS = (((0, QKV), (0, OUT)), ((0, UP),), ((0, DOWN),), ((1, QKV), (1, OUT)), ((1, UP),), ((1, DOWN),))
 F32 = jnp.float32
@@ -33,7 +35,10 @@
         src = lax.broadcasted_iota(jnp.int32, (n, 4 * n), 0)
         dst = lax.broadcasted_iota(jnp.int32, (n, 4 * n), 1)
         pick = (dst == src + pos * n).astype(BF16)
-        out[2 * k:2 * k + 2, :4 * n] = jnp.dot(ref[...], pick, preferred_element_type=F32).astype(BF16)
+        res = jnp.dot(ref[...], pick, preferred_element_type=F32).astype(BF16)
+        for seg in range(4 * n // out.shape[1]):
+            row = 2 * k if seg == 0 else SEG_ROWS + 2 * seg
+            out[row:row + 2, :] = res[:, seg * out.shape[1]:(seg + 1) * out.shape[1]]
 
 
 def _kernel(dims, x_in, *refs):
@@ -157,7 +162,7 @@
             remote(pb, pb, snd_y.at[wid(w)], rec_y.at[wid(w), t - 1, j], y_dev).start()
         if grp + 1 < len(GROUPS):
 
-            @pl.when(t == steps - 1)
+            @pl.when(jnp.logical_and(t == steps - 1, j >= (1 if grp == 0 else 0)))
             def _():
                 own_send(grp + 1, j)
 
@@ -355,8 +360,11 @@
                 for k in (LN1_S, LN1_B, B_OUT, LN2_S, LN2_B, B_DOWN):
                     wv = width // (nd // 4)
                     vrow[2 * k + l:2 * k + l + 1, a * wv:(a + 1) * wv] = s[2 * k + l:2 * k + l + 1, :wv]
-                wv = 3 * width // (nd // 4)
-                vrow[2 * B_QKV + l:2 * B_QKV + l + 1, a * wv:(a + 1) * wv] = s[2 * B_QKV + l:2 * B_QKV + l + 1, :wv]
+                wv = width // (nd // 4)
+                for seg in range(3):
+                    row = l + (2 * B_QKV if seg == 0 else SEG_ROWS + 2 * seg)
+                    at = (3 * a + seg) * wv
+                    vrow[2 * B_QKV + l:2 * B_QKV + l + 1, at:at + wv] = s[row:row + 1, :wv]
         wv = vrow.shape[1] // nd
         for o in range(nd):
             s = vecg[o].astype(F32)
@@ -450,6 +458,7 @@
     pl.semaphore_wait(barrier, 5)
     for j in range(SUB):
         own_send(0, j, (OUT,))
+    own_send(1, 0)
     load_raw(0).wait()
     relay_half(mine)
     _pack(vin, vown)
@@ -525,12 +534,11 @@
     start_group(4)
     begin(qkv1_s)
     run(4, 4, 11, qkv1_n, qkv1_u)
-    run(4, 11, 16, at_n, at_u)
+    run(4, 11, 17, at_n, at_u)
     begin(out1_s)
-    run(4, 16, 19, out1_n, out1_u)
-    run(4, 19, ticks, *ln_unit(1, LN2_S, LN2_B))
-
-    start_group(5)
+    run(4, 17, ticks, out1_n, out1_u)
+
+    start_group(5, ln_unit(1, LN2_S, LN2_B))
     begin(up1_s)
     run(5, 4, 15, up1_n, up1_u)
     slot_ready(0)
@@ -576,6 +584,19 @@
         pltpu.make_async_copy(x.at[msl], out_ref.at[msl], out_sem.at[mb]).wait()
 
 
+def _copy(src, dst, buf, sem_in, sem_out):
+    n = buf.shape[0] // COPIES
+    ins = [pltpu.make_async_copy(src.at[pl.ds(i * n, n)], buf.at[pl.ds(i * n, n)], sem_in.at[i]) for i in range(COPIES)]
+    outs = [pltpu.make_async_copy(buf.at[pl.ds(i * n, n)], dst.at[pl.ds(i * n, n)], sem_out.at[i]) for i in range(COPIES)]
+    for cp in ins:
+        cp.start()
+    for cp, out in zip(ins, outs):
+        cp.wait()
+        out.start()
+    for out in outs:
+        out.wait()
+
+
 def solution(mesh):
     batch_spec = P(('dp', 'fsdp'), None, None)
     vector_spec = P(None, 'fsdp')
@@ -592,7 +613,8 @@
         heads, hd = w_qkv.shape[3], w_qkv.shape[4]
         rows = nimg * seq
         x = images.reshape(rows, width)
-        vw = 4 * b_qkv.shape[1]
+        vw = 4 * b_out.shape[1]
+        vr = -(-(layers * 10) // 16) * 16
         vecs = (ln1_s, ln1_b, b_qkv, b_out, ln2_s, ln2_b, b_up, b_down)
         mats = (w_qkv.reshape(layers, w_qkv.shape[1], 3 * heads, hd), w_out, w_up, w_down)
         cols = (3 * width, width, w_up.shape[2], width)
@@ -602,7 +624,7 @@
         gshapes = [jax.ShapeDtypeStruct((layers, nd * m.shape[1], n), BF16) for m, n in zip(mats, cols)]
         outs = pl.pallas_call(
             functools.partial(_kernel, (ny, nz, heads, hd)),
-            out_shape=[jax.ShapeDtypeStruct((rows, width), BF16), jax.ShapeDtypeStruct((layers * 8, vw), BF16)] + gshapes,
+            out_shape=[jax.ShapeDtypeStruct((rows, width), BF16), jax.ShapeDtypeStruct((vr, vw), BF16)] + gshapes,
             in_specs=[any_spec] + [pl.BlockSpec(memory_space=pltpu.VMEM)] * 8 + [any_spec] * 4,
             out_specs=[any_spec] * 6,
             scratch_shapes=[
@@ -614,9 +636,9 @@
                 pltpu.VMEM((2, width, width // 3), BF16),
                 pltpu.VMEM((2, width, width // 2), BF16),
                 *[pltpu.VMEM((*m.shape[:2], n), BF16) for m, n in zip(mats, cols)],
-                pltpu.VMEM((nd, layers * 8, vw), BF16),
+                pltpu.VMEM((nd, vr, vw), BF16),
                 pltpu.VMEM((layers * 8, w_up.shape[2]), F32),
-                pltpu.VMEM((layers * 8, vw), BF16),
+                pltpu.VMEM((vr, vw), BF16),
                 pltpu.VMEM(mats[0].shape[1:], BF16),
                 pltpu.VMEM((mats[0].shape[1] * 3 * heads, hd), F32),
                 *[dma((nw, nz - 1, SUB))] * 4,
@@ -633,6 +655,13 @@
             ],
             compiler_params=pltpu.CompilerParams(collective_id=0, has_side_effects=True, vmem_limit_bytes=56 * 1024 * 1024),
         )(x, *vecs, *mats)
-        return outs[0].reshape(nimg, seq, width)
+        out = pl.pallas_call(
+            _copy,
+            out_shape=jax.ShapeDtypeStruct((rows, width), BF16),
+            in_specs=[any_spec],
+            out_specs=any_spec,
+            scratch_shapes=[pltpu.VMEM((rows, width), BF16), dma((COPIES,)), dma((COPIES,))],
+        )(outs[0])
+        return out.reshape(nimg, seq, width)
 
     return jax.shard_map(local, mesh=mesh, in_specs=in_specs, out_specs=batch_spec, check_vma=False)

time: 315 us -> 311 us (0.987)
  local copies, waits for them, and re-layouts: 3.22 us -> 0 us
    pallas_call x1, Pallas kernels: 312 us -> 308 us  [local(): pl.pallas_call(functools.partial(_kernel, (ny, nz, heads, hd)), out_shape...]
    unnamed x1 -> x0, local copies, waits for them, and re-layouts: 3.22 us -> none
where the time goes in v3:
time: 311 us
  Pallas kernels  311 us (100%)
    pallas_call x1, Pallas kernels, local(): pl.pallas_call(functools.partial(_kernel, (ny, nz, heads, hd)), out_shape...  308 us

profile of v3, /device:TPU:21, one launch (start us, length us, event | category | flops | bytes accessed | tf_op | source)
XLA Modules:
  0.0 310.7 jit_solution(7980698448707174868)
XLA Ops:
  0.0 308.0 %shard_map.127 = (bf16[768,1536]{1,0:T(8,128)(2,1)}, bf16[32,384]{1,0:T(8,128)(2,1)}, bf16[2,1536,4608]{2,1,0:T(8,128)(2,1)}, bf16[2,1536,1536]{2,1,0:T(8,128)(2...) custom-call(bf16[768,1536]{1,0:T(8,128)(2,1)} %bitcast.3, bf16[2,96]{1,0:T(2,128)(2,1)} %refs_0_.1, ...), custom_call_target="tpu_custom_call" | custom-call | tf_op jit(solution)/shard_map/pallas_call | solution.py:625
  308.0 2.5 shard_map.128
